TPU v7x, 32 devices: a whole 2x2x4 slice. The times are simulated.
32 devices in a mesh: groups: 2 (over x), expert: 8 (over z, y), dp: 2 (over core).
Axes of the slice: x: 2, y: 2, z: 4, core: 2. Of those that a mesh axis runs over, the one named last changes fastest.
Arguments:
- tokens: bfloat16 [128, 2880], P(('groups', 'expert', 'dp')), parts along dimension 0, may hold values from -6 to 6
- norm_gain: bfloat16 [2, 2880], replicated, may hold values from 0.25 to 1.75
- w_gate: bfloat16 [2, 2880, 23040], P(None, None, ('expert', 'dp')), may hold values from -0.109375 to 0.109375
- w_up: bfloat16 [2, 2880, 23040], P(None, None, ('expert', 'dp')), may hold values from -0.109375 to 0.109375
- w_down: bfloat16 [2, 23040, 2880], P(None, ('expert', 'dp')), may hold values from -0.109375 to 0.109375
- routes: int32 [2, 128, 4], P(None, ('groups', 'expert', 'dp')), parts along dimension 1, may hold values from 0 to 7, all different within a row; in each aligned block of 4 rows (0 to 3, 4 to 7, ..., all dimensions but the last counted through in order) at most 3 rows name the same one
- gates: float32 [2, 128, 4], P(None, ('groups', 'expert', 'dp')), parts along dimension 1, may hold values from 0.1 to 1
Outputs:
- mixed: bfloat16 [128, 2880], P(('groups', 'expert', 'dp')), parts along dimension 0
There are 2 independent parts, one for each index of `groups`. A program takes and returns all parts, laid end to end along the dimension named above; an argument that names none is the same for every part. Nothing has to cross between parts.
Inputs may be any that keep to these rules, and one draw needn't show every extreme that they name: `routes`: each token names 4 different experts; among the 4 rows of one device (aligned blocks of a layer) no expert is named more than 3 times, and in every layer some device's block names some expert exactly 3 times.
All inputs are finite; a program needn't handle non-finite values.
Results may differ from a plain program's by a relative error of at most 0.014.
Values may be sent and summed in bfloat16 or wider, within the bound.
A program may use at most 128 MiB of HBM per device.

v0:
```python
import functools

import jax
import jax.numpy as jnp
from jax import lax
from jax.experimental import pallas as pl
from jax.experimental.pallas import tpu as pltpu
from jax.sharding import PartitionSpec as P

MESH = pl.DeviceIdType.MESH
EPS = 1e-05
TILE = 512
PARTS = 3


def col_tiles(start, stop, width):
    tiles = []
    while start < stop:
        tiles.append((start, min(width, stop - start)))
        start += width
    return tiles


def tiled_loop(start, stop, width, body):
    full = (stop - start) // width
    if full > 1:
        @pl.loop(0, full)
        def _(i):
            body(pl.multiple_of(start + i * width, 128), width)
    elif full == 1:
        body(start, width)
    if (stop - start) % width:
        body(start + full * width, (stop - start) % width)


def dot_rows(left, right):
    return lax.dot_general(
        left, right, (((1,), (1,)), ((), ())), preferred_element_type=jnp.float32
    )


def kernel(
    chips, chips_per_expert, tok_ref, gain_ref, wg_hbm, wu_hbm, wd_hbm, routes_ref, gates_ref,
    out_ref,
    wg, wu, wd, gathered, stacked, x_buf, act, y_buf, peer_buf, blocks, back, hidden,
    w_sem, ag_send, ag_recv, fw_send, fw_recv, pr_send, pr_recv, rs_send, rs_recv,
):
    me = lax.axis_index("expert")
    core = lax.axis_index("dp")
    other = 1 - core
    layers, ff, d_model = wg.shape
    rows = tok_ref.shape[0]
    half = chips * rows
    step = -(-d_model // (128 * PARTS)) * 128
    parts = col_tiles(0, d_model, step)

    def weights(layer):
        pairs = ((wg_hbm, wg), (wu_hbm, wu), (wd_hbm, wd))
        return [
            pltpu.make_async_copy(src.at[layer], dst.at[layer], w_sem.at[layer, i])
            for i, (src, dst) in enumerate(pairs)
        ]

    unrolled = chips <= 16 and chips & (chips - 1) == 0

    def mirror(flip):
        total = 0
        bit = 1
        while bit < chips:
            own = lax.rem(me // bit, 2)
            total = total + bit * (1 - own if flip & bit else own)
            bit *= 2
        return total

    mirrored = [mirror(flip) for flip in range(chips - 1, 0, -1)] if unrolled else []

    def each_peer(body):
        for peer in mirrored:
            body(peer)
        if not unrolled:
            @pl.loop(1, chips)
            def _(d):
                body(lax.rem(me + d, chips))

    def each_chip(body):
        if unrolled:
            for slot in range(chips):
                body(slot)
        else:
            pl.loop(0, chips)(body)

    def gather_copy(layer, peer, slot):
        return pltpu.make_async_remote_copy(
            src_ref=gathered.at[layer, core, slot],
            dst_ref=gathered.at[layer, core, slot],
            send_sem=ag_send.at[layer, peer],
            recv_sem=ag_recv.at[layer, slot],
            device_id={"expert": peer},
            device_id_type=MESH,
        )

    def forward_copy(layer, half_idx, slot):
        return pltpu.make_async_remote_copy(
            src_ref=gathered.at[layer, half_idx, slot],
            dst_ref=gathered.at[layer, half_idx, slot],
            send_sem=fw_send.at[layer, slot],
            recv_sem=fw_recv.at[layer, slot],
            device_id={"dp": other},
            device_id_type=MESH,
        )

    def pair_copy(layer, part):
        c0, cw = parts[part]
        return pltpu.make_async_remote_copy(
            src_ref=y_buf.at[layer, other, :, pl.ds(c0, cw)],
            dst_ref=peer_buf.at[layer, :, pl.ds(c0, cw)],
            send_sem=pr_send.at[layer, part],
            recv_sem=pr_recv.at[layer, part],
            device_id={"dp": other},
            device_id_type=MESH,
        )

    def home_copy(layer, part, peer, slot_src, slot_dst):
        c0, cw = parts[part]
        return pltpu.make_async_remote_copy(
            src_ref=blocks.at[layer, slot_src, :, pl.ds(c0, cw)],
            dst_ref=back.at[layer, slot_dst, :, pl.ds(c0, cw)],
            send_sem=rs_send.at[layer, part, peer],
            recv_sem=rs_recv.at[layer, part, slot_dst],
            device_id={"expert": peer},
            device_id_type=MESH,
        )

    for copy in weights(0):
        copy.start()

    barrier = pltpu.get_barrier_semaphore()
    each_peer(
        lambda peer: pl.semaphore_signal(
            barrier, inc=1, device_id={"expert": peer}, device_id_type=MESH
        )
    )
    pl.semaphore_signal(barrier, inc=1, device_id={"dp": other}, device_id_type=MESH)

    hidden[...] = tok_ref[...].astype(jnp.float32)
    gains = gain_ref[...].astype(jnp.float32)
    for layer in range(layers):
        x = hidden[...]
        scale_inv = lax.rsqrt(jnp.mean(x * x, axis=-1, keepdims=True) + EPS)
        normed = (x * scale_inv * gains[layer : layer + 1]).astype(jnp.bfloat16)
        gathered[layer, core, me] = normed
        if layer == 0:
            pl.semaphore_wait(barrier, chips)
        each_peer(lambda peer: gather_copy(layer, peer, me).start())
        forward_copy(layer, core, me).start()
        if layer == 0:
            for later in range(1, layers):
                for copy in weights(later):
                    copy.start()

        def pass_on(peer):
            gather_copy(layer, peer, peer).wait_recv()
            forward_copy(layer, core, peer).start()

        each_peer(pass_on)

        each_chip(lambda slot: forward_copy(layer, other, slot).wait_recv())

        per = 8 // rows
        for h in range(2):
            @pl.loop(0, chips // per)
            def _(q):
                stacked[h, q] = jnp.concatenate(
                    [gathered[layer, h, q * per + i].astype(jnp.float32) for i in range(per)], axis=0
                )
        x_buf[...] = stacked[...].reshape(2 * half, d_model).astype(jnp.bfloat16)

        w_gate, w_up, w_down = weights(layer)
        w_gate.wait()
        w_up.wait()

        def up_tile(c0, cw):
            cols = pl.ds(c0, cw)
            g = dot_rows(wg[layer, cols, :], x_buf[...]).T
            u = dot_rows(wu[layer, cols, :], x_buf[...]).T
            act[:, cols] = (g * jax.nn.sigmoid(1.702 * g) * (u + 1.0)).astype(jnp.bfloat16)

        tiled_loop(0, ff, TILE, up_tile)
        w_down.wait()

        def down_tile(c0, cw):
            cols = pl.ds(c0, cw)
            y = jnp.dot(act[...], wd[layer, :, cols], preferred_element_type=jnp.float32)
            y_buf[layer, :, :, cols] = y.reshape(2, half, cw)

        def send_home(part):
            c0, cw = parts[part]
            cols = pl.ds(c0, cw)
            pair_copy(layer, part).wait_recv()

            @pl.loop(0, chips // per)
            def _(q):
                group = pl.ds(pl.multiple_of(q * 8, 8), 8)
                total = y_buf[layer, core, group, cols] + peer_buf[layer, group, cols]
                for i in range(per):
                    blocks[layer, q * per + i, :, cols] = total[i * rows : (i + 1) * rows].astype(
                        jnp.bfloat16
                    )

            each_peer(lambda peer: home_copy(layer, part, peer, peer, me).start())

        for part, (c0, cw) in enumerate(parts):
            tiled_loop(c0, c0 + cw, TILE, down_tile)
            pair_copy(layer, part).start()
            if part > 0:
                send_home(part - 1)
        send_home(len(parts) - 1)

        routes = routes_ref[layer]
        gates = gates_ref[layer]

        def weight_of(chip):
            expert = chip // chips_per_expert
            return jnp.sum(jnp.where(routes == expert, gates, 0.0), axis=1, keepdims=True)

        hidden[...] += weight_of(me) * blocks[layer, me].astype(jnp.float32)

        def take(peer):
            for part in range(len(parts)):
                home_copy(layer, part, peer, peer, peer).wait_recv()
            hidden[...] += weight_of(peer) * back[layer, peer].astype(jnp.float32)

        each_peer(take)
        result = hidden[...].astype(jnp.bfloat16)
        if layer + 1 < layers:
            hidden[...] = result.astype(jnp.float32)
        else:
            out_ref[...] = result

    for layer in range(layers):
        each_chip(lambda slot: forward_copy(layer, core, slot).wait_send())

        def sent(peer):
            gather_copy(layer, peer, me).wait_send()
            for part in range(len(parts)):
                home_copy(layer, part, peer, peer, me).wait_send()

        each_peer(sent)
        for part in range(len(parts)):
            pair_copy(layer, part).wait_send()


def on_device(tokens, norm_gain, w_gate, w_up, w_down, routes, gates, *, expert_total_of):
    chips = lax.axis_size("expert")
    cores = lax.axis_size("dp")
    rows, d_model = tokens.shape
    layers, _, ff = w_gate.shape
    expert_total = expert_total_of(d_model, ff, chips * cores)
    half = chips * rows
    vmem = pl.BlockSpec(memory_space=pltpu.VMEM)
    hbm = pl.BlockSpec(memory_space=pl.ANY)
    dma = pltpu.SemaphoreType.DMA
    parts = len(col_tiles(0, d_model, -(-d_model // (128 * PARTS)) * 128))
    bf16, f32 = jnp.bfloat16, jnp.float32
    return pl.pallas_call(
        functools.partial(kernel, chips, chips // expert_total),
        out_shape=jax.ShapeDtypeStruct(tokens.shape, tokens.dtype),
        in_specs=[vmem, vmem, hbm, hbm, hbm, vmem, vmem],
        out_specs=vmem,
        scratch_shapes=[
            pltpu.VMEM((layers, ff, d_model), bf16),
            pltpu.VMEM((layers, ff, d_model), bf16),
            pltpu.VMEM((layers, ff, d_model), bf16),
            pltpu.VMEM((layers, 2, chips, rows, d_model), bf16),
            pltpu.VMEM((2, half // 8, 8, d_model), f32),
            pltpu.VMEM((2 * half, d_model), bf16),
            pltpu.VMEM((2 * half, ff), bf16),
            pltpu.VMEM((layers, 2, half, d_model), f32),
            pltpu.VMEM((layers, half, d_model), f32),
            pltpu.VMEM((layers, chips, rows, d_model), bf16),
            pltpu.VMEM((layers, chips, rows, d_model), bf16),
            pltpu.VMEM((rows, d_model), f32),
            dma((layers, 3)),
            dma((layers, chips)),
            dma((layers, chips)),
            dma((layers, chips)),
            dma((layers, chips)),
            dma((layers, parts)),
            dma((layers, parts)),
            dma((layers, parts, chips)),
            dma((layers, parts, chips)),
        ],
        compiler_params=pltpu.CompilerParams(
            collective_id=0, has_side_effects=True, vmem_limit_bytes=67043328
        ),
    )(
        tokens,
        norm_gain,
        jnp.swapaxes(w_gate, 1, 2),
        jnp.swapaxes(w_up, 1, 2),
        w_down,
        routes,
        gates,
    )


def solution(mesh):
    def expert_total_of(d_model, ff, devices):
        return devices * ff // d_model

    return jax.shard_map(
        functools.partial(on_device, expert_total_of=expert_total_of),
        mesh=mesh,
        in_specs=(
            P(("groups", "expert", "dp"), None),
            P(),
            P(None, None, ("expert", "dp")),
            P(None, None, ("expert", "dp")),
            P(None, ("expert", "dp"), None),
            P(None, ("groups", "expert", "dp"), None),
            P(None, ("groups", "expert", "dp"), None),
        ),
        out_specs=P(("groups", "expert", "dp"), None),
        check_vma=False,
    )
```

profile of v0, /device:TPU:0, one launch (start us, length us, event | category | flops | bytes accessed | tf_op | source)
XLA Modules:
  0.0 50.8 jit_solution(18015996406217592876)
XLA Ops:
  0.0 49.5 %shard_map.73 = bf16[4,2880]{1,0:T(4,128)(2,1)} custom-call(bf16[4,2880]{1,0:T(4,128)(2,1)} %tok_ref.1, bf16[2,2880]{1,0:T(2,128)(2,1)} %gain_ref.1, bf16[2,1440,2880]{2,1,0:T(8,128)(2,1)} %bitcast.2, bf16[2,1440,2880]{2,1,0:T(8,128)(2,1)} %bitcast.3, bf16[2,1440,2880]{2,1,0:T(8,128)(2,1)} %wd_hbm.1, s32[2,4,4]{2,1,0:T(4,128)} %routes_ref.1, ...), custom_call_target="tpu_custom_call" | custom-call | tf_op jit(solution)/shard_map/pallas_call | solution.py:265
  49.5 1.4 %copy.9 = bf16[4,2880]{1,0:T(4,128)(2,1)} copy(bf16[4,2880]{1,0:T(4,128)(2,1)} %shard_map.73) | data formatting | bytes 46080
where the time goes:
time: 51.1 us; the launch traced here: 50.8 us
  Pallas kernels  49.5 us (97%)
  local copies, waits for them, and re-layouts  1.35 us (3%)
    pallas_call x1, Pallas kernels, on_device(): pl.pallas_call(functools.partial(kernel, chips, chips // expert_total), o...  49.5 us
    unnamed x1, local copies, waits for them, and re-layouts  1.35 us

commit v1 on v0

--- a/solution.py
+++ b/solution.py
@@ -11,6 +11,7 @@
 EPS = 1e-05
 TILE = 512
 PARTS = 3
+MXU = 256
 
 
 def col_tiles(start, stop, width):
@@ -39,27 +40,136 @@
     )
 
 
+def tiled(chips, rows, d_model, ff):
+    tokens = 2 * chips * rows
+    blocks = -(-ff // MXU)
+    tails = (d_model % MXU, ff % MXU)
+    return (
+        tokens % 16 == 0
+        and blocks * (tokens // 4) <= 256
+        and all(tail and tail % 16 == 0 for tail in tails)
+        and tails[0] <= 128
+    )
+
+
+def filled(block, size):
+    short = size - block.shape[0]
+    if short == 0:
+        return block
+    return jnp.concatenate([block, jnp.zeros((short, block.shape[1]), block.dtype)], axis=0)
+
+
 def kernel(
     chips, chips_per_expert, tok_ref, gain_ref, wg_hbm, wu_hbm, wd_hbm, routes_ref, gates_ref,
     out_ref,
     wg, wu, wd, gathered, stacked, x_buf, act, y_buf, peer_buf, blocks, back, hidden,
     w_sem, ag_send, ag_recv, fw_send, fw_recv, pr_send, pr_recv, rs_send, rs_recv,
+    *tails, accs=None,
 ):
     me = lax.axis_index("expert")
     core = lax.axis_index("dp")
     other = 1 - core
-    layers, ff, d_model = wg.shape
+    layers, ff, d_model = wd_hbm.shape
     rows = tok_ref.shape[0]
+    fast = accs is not None
+    whole = d_model // MXU * MXU
+    rest = d_model - whole
+    strips = -(-ff // MXU)
     half = chips * rows
     step = -(-d_model // (128 * PARTS)) * 128
     parts = col_tiles(0, d_model, step)
 
+    if fast:
+        wg_raw, wu_raw, wd_raw, wg_rest, wu_rest, wd_rest = tails
+        ups = ((wg_hbm, wg, wg_raw, wg_rest), (wu_hbm, wu, wu_raw, wu_rest))
+
+    def strip_copy(layer, i, f):
+        src, dst = ups[i][:2]
+        height = pl.ds(f * MXU, min(MXU, ff - f * MXU))
+        return pltpu.make_async_copy(
+            src.at[layer, height, pl.ds(0, whole)], dst.at[layer, height, :], w_sem.at[layer, i, f]
+        )
+
+    def rest_copy(layer, i):
+        src, raw = (ups[0][0], wg_raw) if i == 0 else (ups[1][0], wu_raw) if i == 1 else (wd_hbm, wd_raw)
+        return pltpu.make_async_copy(
+            src.at[layer, :, pl.ds(whole, rest)],
+            raw.at[layer, pl.ds(0, ff), :],
+            w_sem.at[layer, i, strips],
+        )
+
+    def down_copy(layer):
+        return pltpu.make_async_copy(
+            wd_hbm.at[layer, :, pl.ds(0, whole)], wd.at[layer], w_sem.at[layer, 2, 0]
+        )
+
     def weights(layer):
+        if fast:
+            return (
+                [rest_copy(layer, i) for i in range(2)]
+                + [strip_copy(layer, i, f) for f in range(strips) for i in range(2)]
+                + [rest_copy(layer, 2), down_copy(layer)]
+            )
         pairs = ((wg_hbm, wg), (wu_hbm, wu), (wd_hbm, wd))
         return [
             pltpu.make_async_copy(src.at[layer], dst.at[layer], w_sem.at[layer, i])
             for i, (src, dst) in enumerate(pairs)
         ]
+
+    def turn(layer, i, f):
+        _, dst, raw, turned = ups[i]
+        strip_copy(layer, i, f).wait()
+        if f == 0:
+            rest_copy(layer, i).wait()
+        height = pl.ds(f * MXU, MXU)
+        for k in range(whole // MXU):
+            cols = pl.ds(k * MXU, MXU)
+            dst[layer, height, cols] = dst[layer, height, cols].T
+        turned[layer, :, height] = raw[layer, height, :].T
+
+    def turn_all(layer, pieces):
+        for i, f in pieces:
+            turn(layer, i, f)
+
+    def pad_down(layer):
+        rest_copy(layer, 2).wait()
+        wd_rest[layer] = jnp.zeros(wd_rest.shape[1:], wd_rest.dtype)
+        wd_rest[layer, pl.ds(0, ff), pl.ds(0, rest)] = wd_raw[layer, pl.ds(0, ff), :]
+
+    def multiply_up(layer, k_range, finish):
+        for f in range(strips):
+            height = pl.ds(f * MXU, MXU)
+            for k in k_range:
+                left = x_buf[:, pl.ds(k * MXU, MXU)]
+                for i in range(2):
+                    _, dst, _, turned = ups[i]
+                    if (k + 1) * MXU <= whole:
+                        tile = dst[layer, height, pl.ds(k * MXU, MXU)]
+                    else:
+                        tile = filled(turned[layer, :, height], MXU)
+                    register = (f * len(k_range) + k) % 2
+                    pltpu.matmul_push_rhs(tile, staging_register=register, mxu_index=i)
+                    pltpu.matmul_acc_lhs(accs[i][f], left, load_staged_rhs=register)
+            if finish:
+                g = pltpu.matmul_pop(accs[0][f])
+                u = pltpu.matmul_pop(accs[1][f])
+                value = g * jax.nn.sigmoid(1.702 * g) * (u + 1.0)
+                if (f + 1) * MXU > ff:
+                    place = lax.broadcasted_iota(jnp.int32, value.shape, 1)
+                    value = jnp.where(place < ff - f * MXU, value, 0.0)
+                act[:, height] = value.astype(jnp.bfloat16)
+
+    def multiply_down(layer, n):
+        acc = accs[n % 2][n // 2 % strips]
+        cols = pl.ds(n * MXU, MXU)
+        for k in range(strips):
+            height = pl.ds(k * MXU, min(MXU, ff - k * MXU))
+            tile = wd[layer, height, cols] if (n + 1) * MXU <= whole else wd_rest[layer, height, :]
+            pltpu.matmul_push_rhs(filled(tile, MXU), staging_register=k % 2, mxu_index=n % 2)
+            pltpu.matmul_acc_lhs(acc, act[:, pl.ds(k * MXU, MXU)], load_staged_rhs=k % 2)
+        y = pltpu.matmul_pop(acc)
+        width = min(MXU, d_model - n * MXU)
+        y_buf[layer, :, :, pl.ds(n * MXU, width)] = y.reshape(2, half, MXU)[:, :, :width]
 
     unrolled = chips <= 16 and chips & (chips - 1) == 0
 
@@ -157,6 +267,9 @@
             for later in range(1, layers):
                 for copy in weights(later):
                     copy.start()
+            if fast:
+                turn_all(0, [(i, f) for f in range(strips) for i in range(2)])
+                pad_down(0)
 
         def pass_on(peer):
             gather_copy(layer, peer, peer).wait_recv()
@@ -173,11 +286,14 @@
                 stacked[h, q] = jnp.concatenate(
                     [gathered[layer, h, q * per + i].astype(jnp.float32) for i in range(per)], axis=0
                 )
-        x_buf[...] = stacked[...].reshape(2 * half, d_model).astype(jnp.bfloat16)
-
-        w_gate, w_up, w_down = weights(layer)
-        w_gate.wait()
-        w_up.wait()
+        x_buf[:, pl.ds(0, d_model)] = stacked[...].reshape(2 * half, d_model).astype(jnp.bfloat16)
+        if fast:
+            short = x_buf.shape[1] - d_model
+            x_buf[:, pl.ds(d_model, short)] = jnp.zeros((2 * half, short), jnp.bfloat16)
+        else:
+            w_gate, w_up, w_down = weights(layer)
+            w_gate.wait()
+            w_up.wait()
 
         def up_tile(c0, cw):
             cols = pl.ds(c0, cw)
@@ -185,8 +301,12 @@
             u = dot_rows(wu[layer, cols, :], x_buf[...]).T
             act[:, cols] = (g * jax.nn.sigmoid(1.702 * g) * (u + 1.0)).astype(jnp.bfloat16)
 
-        tiled_loop(0, ff, TILE, up_tile)
-        w_down.wait()
+        if fast:
+            multiply_up(layer, range(x_buf.shape[1] // MXU), True)
+            down_copy(layer).wait()
+        else:
+            tiled_loop(0, ff, TILE, up_tile)
+            w_down.wait()
 
         def down_tile(c0, cw):
             cols = pl.ds(c0, cw)
@@ -210,11 +330,18 @@
             each_peer(lambda peer: home_copy(layer, part, peer, peer, me).start())
 
         for part, (c0, cw) in enumerate(parts):
-            tiled_loop(c0, c0 + cw, TILE, down_tile)
+            if fast:
+                for n in range(c0 // MXU, -(-(c0 + cw) // MXU)):
+                    multiply_down(layer, n)
+            else:
+                tiled_loop(c0, c0 + cw, TILE, down_tile)
             pair_copy(layer, part).start()
             if part > 0:
                 send_home(part - 1)
         send_home(len(parts) - 1)
+        if fast and layer + 1 < layers:
+            turn_all(layer + 1, [(i, f) for f in range(strips) for i in range(2)])
+            pad_down(layer + 1)
 
         routes = routes_ref[layer]
         gates = gates_ref[layer]
@@ -262,25 +389,45 @@
     dma = pltpu.SemaphoreType.DMA
     parts = len(col_tiles(0, d_model, -(-d_model // (128 * PARTS)) * 128))
     bf16, f32 = jnp.bfloat16, jnp.float32
+    fast = tiled(chips, rows, d_model, ff)
+    strips = -(-ff // MXU)
+    whole, high = d_model // MXU * MXU, strips * MXU
+    rest, wide = d_model - whole, -(-d_model // MXU) * MXU
+    body = functools.partial(kernel, chips, chips // expert_total)
+    if fast:
+        ups = [pltpu.VMEM((layers, high, whole), bf16)] * 2 + [pltpu.VMEM((layers, ff, whole), bf16)]
+        tails = [pltpu.VMEM((layers, high, rest), bf16)] * 3
+        tails += [pltpu.VMEM((layers, rest, high), bf16)] * 2 + [pltpu.VMEM((layers, high, MXU), bf16)]
+        x_shape, act_shape, w_sems = (2 * half, wide), (2 * half, high), (layers, 3, strips + 1)
+
+        def body(*refs):
+            each = [pltpu.ACC(i)((2 * half, MXU), f32) for i in range(2) for _ in range(strips)]
+            pl.run_scoped(
+                lambda *accs: kernel(
+                    chips, chips // expert_total, *refs, accs=(accs[:strips], accs[strips:])
+                ),
+                *each,
+            )
+    else:
+        ups, tails = [pltpu.VMEM((layers, ff, d_model), bf16)] * 3, []
+        x_shape, act_shape, w_sems = (2 * half, d_model), (2 * half, ff), (layers, 3)
     return pl.pallas_call(
-        functools.partial(kernel, chips, chips // expert_total),
+        body,
         out_shape=jax.ShapeDtypeStruct(tokens.shape, tokens.dtype),
         in_specs=[vmem, vmem, hbm, hbm, hbm, vmem, vmem],
         out_specs=vmem,
         scratch_shapes=[
-            pltpu.VMEM((layers, ff, d_model), bf16),
-            pltpu.VMEM((layers, ff, d_model), bf16),
-            pltpu.VMEM((layers, ff, d_model), bf16),
+            *ups,
             pltpu.VMEM((layers, 2, chips, rows, d_model), bf16),
             pltpu.VMEM((2, half // 8, 8, d_model), f32),
-            pltpu.VMEM((2 * half, d_model), bf16),
-            pltpu.VMEM((2 * half, ff), bf16),
+            pltpu.VMEM(x_shape, bf16),
+            pltpu.VMEM(act_shape, bf16),
             pltpu.VMEM((layers, 2, half, d_model), f32),
             pltpu.VMEM((layers, half, d_model), f32),
             pltpu.VMEM((layers, chips, rows, d_model), bf16),
             pltpu.VMEM((layers, chips, rows, d_model), bf16),
             pltpu.VMEM((rows, d_model), f32),
-            dma((layers, 3)),
+            dma(w_sems),
             dma((layers, chips)),
             dma((layers, chips)),
             dma((layers, chips)),
@@ -289,6 +436,7 @@
             dma((layers, parts)),
             dma((layers, parts, chips)),
             dma((layers, parts, chips)),
+            *tails,
         ],
         compiler_params=pltpu.CompilerParams(
             collective_id=0, has_side_effects=True, vmem_limit_bytes=67043328

time: 51.1 us -> 50 us (0.978)
  Pallas kernels: 49.5 us -> 48.4 us
    pallas_call x1, Pallas kernels: 49.5 us -> 48.4 us  [on_device(): pl.pallas_call(body, out_shape=jax.ShapeDtypeStruct(tokens.shape, tokens....]
where the time goes in v1:
time: 50 us; the launch traced here: 49.8 us
  Pallas kernels  48.4 us (97%)
  local copies, waits for them, and re-layouts  1.35 us (3%)
    pallas_call x1, Pallas kernels, on_device(): pl.pallas_call(body, out_shape=jax.ShapeDtypeStruct(tokens.shape, tokens....  48.4 us
    unnamed x1, local copies, waits for them, and re-layouts  1.35 us

profile of v1, /device:TPU:0, one launch (start us, length us, event | category | flops | bytes accessed | tf_op | source)
XLA Modules:
  0.0 49.8 jit_solution(17655127025186105561)
XLA Ops:
  0.0 48.4 %shard_map.73 = bf16[4,2880]{1,0:T(4,128)(2,1)} custom-call(bf16[4,2880]{1,0:T(4,128)(2,1)} %refs_0_.1, bf16[2,2880]{1,0:T(2,128)(2,1)} %refs_1_.1, bf16[2,1440,2880]{2,1,0:T(8,128)(2,1)} %bitcast.2, bf16[2,1440,2880]{2,1,0:T(8,128)(2,1)} %bitcast.3, bf16[2,1440,2880]{2,1,0:T(8,128)(2,1)} %refs_4_.1, s32[2,4,4]{2,1,0:T(4,128)} %refs_5_.1, f32[2,4,4]{2,1,0:T(4,128)} %refs_6_.1), custom_call_target="tpu_custom_call" | custom-call | tf_op jit(solution)/shard_map/pallas_call | solution.py:414
  48.4 1.4 %copy.9 = bf16[4,2880]{1,0:T(4,128)(2,1)} copy(bf16[4,2880]{1,0:T(4,128)(2,1)} %shard_map.73) | data formatting | bytes 46080
